TPU v7x, 32 devices: a whole 2x2x4 slice. The times are simulated.
32 devices in a mesh: snap: 2 (over y), row: 8 (over z, x), col: 2 (over core).
Axes of the slice: x: 2, y: 2, z: 4, core: 2. Of those that a mesh axis runs over, the one named last changes fastest.
Arguments:
- density: bfloat16 [8192, 1024], P(('snap', 'row'), 'col'), parts along dimension 0, may hold values from -0.5 to 2
- pattern: int32 [256, 32], P(('snap', 'row'), 'col'), parts along dimension 0, may hold values 0 or 1
- filter_mask: int32 [256, 32], P(('snap', 'row')), parts along dimension 0, may hold values 0 or 1
Outputs:
- purified: bfloat16 [8192, 1024], P(('snap', 'row'), 'col'), parts along dimension 0
- traces: float32 [4], P('snap'), parts along dimension 0
There are 2 independent parts, one for each index of `snap`. A program takes and returns all parts, laid end to end along the dimension named above; each array names one. Nothing has to cross between parts.
All inputs are finite; a program needn't handle non-finite values. No bound on the sum of `pattern` or of `filter_mask` on one device may be relied on, other than what follows from the above.
Results may differ from a plain program's by a relative error of at most 0.006.
Values may be sent and summed in bfloat16 or wider, within the bound.
A program may use at most 64 MiB of HBM per device.

v0:
```python
import jax
import jax.numpy as jnp
from jax import lax
from jax.sharding import PartitionSpec as P

BLK = 32


def extended_2(value, sides, width):
    for axis, dim in sides:
        size, length = (lax.axis_size(axis), value.shape[dim])
        up = [(i, (i + 1) % size) for i in range(size - 1)]
        down = [(j, i) for i, j in up]
        last = lax.slice_in_dim(value, length - width, length, axis=dim)
        leading = lax.slice_in_dim(value, 0, width, axis=dim)
        before = lax.ppermute(last, axis, up)
        after = lax.ppermute(leading, axis, down)
        value = jnp.concatenate([before, value, after], axis=dim)
    return value


def valid_slots(first_row, row_count, first_slot, slot_count, half_band, block_total):
    row_index = first_row + jnp.arange(row_count, dtype=jnp.int32)
    slot_index = first_slot + jnp.arange(slot_count, dtype=jnp.int32)
    column_index = row_index[:, None] + slot_index[None, :] - half_band
    return ((column_index >= 0) & (column_index < block_total)).astype(jnp.int32)


def expand_mask(values, keep_mask):
    block_rows = keep_mask.shape[0]
    slot_count = keep_mask.shape[1]
    blocks = values.reshape(block_rows, BLK, slot_count, BLK)
    blocks = blocks * keep_mask.astype(values.dtype)[:, None, :, None]
    return blocks.reshape(block_rows * BLK, slot_count * BLK)


def shift_slots(segment, moved):
    height = segment.shape[0]
    if moved > 0:
        return jnp.concatenate(
            [
                jnp.zeros((height, moved * BLK), segment.dtype),
                segment[:, : segment.shape[1] - moved * BLK],
            ],
            1,
        )
    if moved < 0:
        return jnp.concatenate(
            [segment[:, -moved * BLK :], jnp.zeros((height, -moved * BLK), segment.dtype)], 1
        )
    return segment


def band_part(left, extended, first_slot, column_slots, slot_count, half_band):
    block_rows = left.shape[0] // BLK
    byte_limit = 4 * 1024 * 1024
    group_rows = 1
    for candidate in (8, 4, 2):
        if (
            block_rows % candidate == 0
            and candidate * slot_count * BLK * column_slots * BLK * 2 <= byte_limit
        ):
            group_rows = candidate
            break

    def one_group(group):
        first = group * group_rows
        stacked = []
        for offset in range(slot_count):
            segment = lax.dynamic_slice_in_dim(
                extended, (first + offset) * BLK, group_rows * BLK, 0
            )
            segment = shift_slots(segment, offset - half_band)
            segment = lax.dynamic_slice_in_dim(segment, first_slot * BLK, column_slots * BLK, 1)
            stacked.append(segment.reshape(group_rows, BLK, column_slots * BLK))
        gathered = jnp.stack(stacked, 1).reshape(group_rows, slot_count * BLK, column_slots * BLK)
        left_rows = lax.dynamic_slice_in_dim(left, first * BLK, group_rows * BLK, 0).reshape(
            group_rows, BLK, slot_count * BLK
        )
        result = jnp.einsum("gak,gkn->gan", left_rows, gathered, preferred_element_type=jnp.float32)
        return result.reshape(group_rows * BLK, column_slots * BLK)

    result = lax.map(one_group, jnp.arange(block_rows // group_rows, dtype=jnp.int32))
    return result.reshape(block_rows * BLK, column_slots * BLK)


def diagonal_sum(values, chosen):
    block_rows = values.shape[0] // BLK
    slot_total = values.shape[1] // BLK
    diagonal = jnp.diagonal(values.reshape(block_rows, BLK, slot_total, BLK), axis1=1, axis2=3)
    return jnp.sum(diagonal.astype(jnp.float32) * chosen[None, :, None])


def slot_products(
    full_rows, extended, own_filter, first_slot, half_slots, slot_count, half_band, collect
):
    square = band_part(full_rows, extended, first_slot, half_slots, slot_count, half_band)
    squared = expand_mask(square, own_filter).astype(jnp.bfloat16)
    squared_rows = collect(squared)
    cube = band_part(squared_rows, extended, first_slot, half_slots, slot_count, half_band)
    purified = (3.0 * squared.astype(jnp.float32) - 2.0 * expand_mask(cube, own_filter)).astype(
        jnp.bfloat16
    )
    return (purified, squared)


def per_device(density, pattern, filter_mask):
    half_slots = density.shape[1] // BLK
    slot_count = 2 * half_slots
    block_rows = density.shape[0] // BLK
    col_id = lax.axis_index("col")
    row_id = lax.axis_index("row")
    block_total = block_rows * lax.axis_size("row")
    first_slot = col_id * half_slots
    own_valid = valid_slots(
        row_id * block_rows, block_rows, first_slot, half_slots, half_slots, block_total
    )
    kept = expand_mask(density, pattern * own_valid)
    chosen = (first_slot + jnp.arange(half_slots, dtype=jnp.int32) == half_slots).astype(
        jnp.float32
    )
    trace_kept = diagonal_sum(kept, chosen)
    total_kept = lax.psum(trace_kept, ("row", "col"))
    own_filter = lax.dynamic_slice_in_dim(filter_mask, first_slot, half_slots, 1) * own_valid
    rim_rows = extended_2(kept, (("row", 0),), half_slots * BLK)
    extended = lax.all_gather(rim_rows, "col", axis=1, tiled=True)
    full_rows = extended[half_slots * BLK : half_slots * BLK + block_rows * BLK]

    def collect_half(squared):
        return lax.all_gather(squared, "col", axis=1, tiled=True)

    purified, squared = slot_products(
        full_rows,
        extended,
        own_filter,
        first_slot,
        half_slots,
        slot_count,
        half_slots,
        collect_half,
    )
    trace_squared = diagonal_sum(squared, chosen)
    total_squared = lax.psum(trace_squared, ("row", "col"))
    order_total = block_total * BLK
    traces = jnp.stack([total_kept, total_squared]) / order_total
    return (purified, traces)


def solution(mesh):
    return jax.shard_map(
        per_device,
        mesh=mesh,
        in_specs=(P(("snap", "row"), "col"), P(("snap", "row"), "col"), P(("snap", "row"), None)),
        out_specs=(P(("snap", "row"), "col"), P("snap")),
        check_vma=False,
    )
```

profile of v0, /device:TPU:0, one launch (start us, length us, event | category | flops | bytes accessed | tf_op | source)
XLA Modules:
  0.0 517.6 jit_solution(5589783563380693730)
XLA Ops:
  10.6 4.9 collective-permute-start
  16.8 21.1 %collective-permute-done = bf16[512,512]{1,0:T(8,128)(2,1)S(1)} collective-permute-done((bf16[512,512]{1,0:T(8,128)(2,1)S(1)}, bf16[512,512]{1,0:T(8,128)(2,1)S(1)}, u32[]{:S(2)}, u32[]{:S(2)}) %collective-permute-start) | collective-permute-done | bytes 524320 | tf_op jit(solution)/shard_map/ppermute | solution.py:16
  40.5 4.3 copy.7
  44.8 2.4 mul.808.clone
  47.2 4.7 mul.809
  57.1 199.7 %while.26 = (s32[]{:T(128)}, f32[4,128,512]{2,1,0:T(8,128)}, s32[4]{0:T(128)S(1)}, bf16[512,1024]{1,0:T(8,128)(2,1)}, bf16[1536,1024]{1,0:T(8,128)(2,1)}, /*inde...) while((s32[]{:T(128)}, f32[4,128,512]{2,1,0:T(8,128)}, ...), condition=%wide.region_1.2_spmd, body=%wide.region_0.1_spmd.sunk | while | flops 134217904 | bytes 56200764 | solution.py:83
  103.3 3.0 fusion.27
  153.2 3.0 fusion.27
  203.1 3.0 fusion.27
  253.0 3.0 fusion.27
  256.7 2.5 fusion.4
  259.2 4.6 multiply_bitcast_fusion
  263.8 2.8 gather_fusion
  266.7 2.7 reshape_reshape.10
  269.4 7.3 %copy.8 = f32[16,32,16,32]{2,0,3,1:T(8,128)} copy(f32[16,32,16,32]{3,2,1,0:T(8,128)} %reshape_reshape.10) | data formatting | bytes 2097152 | tf_op jit(solution)/shard_map/reshape;reshape | solution.py:32
  276.6 6.8 %fusion = bf16[16,16,32,32]{1,0,3,2:T(8,128)(2,1)} fusion(f32[16,32,16,32]{2,0,3,1:T(8,128)} %copy.8, f32[16,16]{1,0:T(8,128)S(1)} %get-tuple-element.403), kind=kLoop, calls=%fused_computation.163 | loop fusion | flops 524288 | bytes 1573888 | tf_op jit(solution)/shard_map/jit(diagonal)/transpose | solution.py:90
  283.4 2.8 gather_fusion.1
  287.0 34.8 %all-reduce.62 = (f32[1]{0:T(128)}, f32[1]{0:T(128)}) all-reduce(f32[1]{0:T(128)} %bitcast.140, f32[1]{0:T(128)} %bitcast.138), channel_id=1, replica_groups=mesh['snap'=2,'row'=8,'col'=2] {'row','col'}, use_global_device_ids=true, to_apply=%region_7.8 | all-reduce | flops 2 | bytes 16 | tf_op jit(solution)/shard_map/psum | solution.py:143
  324.8 183.3 %while.27 = (s32[]{:T(128)}, f32[4,128,512]{2,1,0:T(8,128)}, s32[4]{0:T(128)S(1)}, bf16[512,1024]{1,0:T(8,128)(2,1)}, bf16[1536,1024]{1,0:T(8,128)(2,1)S(1)}, /*...) while((s32[]{:T(128)}, f32[4,128,512]{2,1,0:T(8,128)}, ...), condition=%wide.region_3.4_spmd, body=%wide.region_2.3_spmd.sunk | while | flops 134217904 | bytes 43617860 | solution.py:83
  366.9 3.0 fusion.31
  412.7 3.0 fusion.31
  458.5 3.0 fusion.31
  504.3 3.0 fusion.31
  508.0 2.8 fusion.3
  (734 shorter events, 361.9 us)
Async XLA Ops:
  7.2 46.5 %all-gather.3.cloned.1.call-start = ((), (), s32[]{:S(2)}) async-start(), calls=%async_computation | async-start | bytes 4718592 | tf_op jit(solution)/shard_map/all_gather | solution.py:126
  10.6 27.3 %collective-permute-start = (bf16[512,512]{1,0:T(8,128)(2,1)S(1)}, bf16[512,512]{1,0:T(8,128)(2,1)S(1)}, u32[]{:S(2)}, u32[]{:S(2)}) collective-permute-start(bf16[512,512]{1,0:T(8,128)(2,1)S(1)} %mul.805), channel_id=1, source_target_pairs={{0,2},{2,4},{4,6},{6,8},{8,10},{10,12},{12,14},{1,3},{3,5},{5,7},{... | collective-permute-start | bytes 1572872 | tf_op jit(solution)/shard_map/ppermute | solution.py:16
  15.5 22.4 %collective-permute-start.1 = (bf16[512,512]{1,0:T(8,128)(2,1)S(1)}, bf16[512,512]{1,0:T(8,128)(2,1)S(1)}, u32[]{:S(2)}, u32[]{:S(2)}) collective-permute-start(bf16[512,512]{1,0:T(8,128)(2,1)S(1)} %mul.805), channel_id=1, source_target_pairs={{2,0},{4,2},{6,4},{8,6},{10,8},{12,10},{14,12},{3,1},{5,3},{7,5},{... | collective-permute-start | bytes 1572872 | tf_op jit(solution)/shard_map/ppermute | solution.py:17
  39.2 284.5 %all-gather.5.cloned.1.call-start = ((), (), s32[]{:S(2)}) async-start(), calls=%async_computation.1 | async-start | bytes 1572864 | tf_op jit(solution)/shard_map/all_gather | solution.py:130
  57.1 13.0 %copy-start = (bf16[1536,1024]{1,0:T(8,128)(2,1)S(1)}, bf16[1536,1024]{1,0:T(8,128)(2,1)}, u32[]{:S(2)}) copy-start(bf16[1536,1024]{1,0:T(8,128)(2,1)} %get-tuple-element.866) | copy-start | bytes 9437188 | tf_op jit(solution)/shard_map/while
  88.1 12.7 %copy-start.14 = (bf16[128,576]{1,0:T(8,128)(2,1)S(1)}, bf16[128,576]{1,0:T(8,128)(2,1)}, u32[]{:S(2)}) copy-start(bf16[128,576]{1,0:T(8,128)(2,1)} %get-tuple-element.668) | copy-start | bytes 442372 | tf_op jit(solution)/shard_map/while
  88.1 12.6 %copy-start.16 = (bf16[128,544]{1,0:T(8,128)(2,1)S(1)}, bf16[128,544]{1,0:T(8,128)(2,1)}, u32[]{:S(2)}) copy-start(bf16[128,544]{1,0:T(8,128)(2,1)} %get-tuple-element.667) | copy-start | bytes 417796 | tf_op jit(solution)/shard_map/while
  107.0 13.0 %copy-start = (bf16[1536,1024]{1,0:T(8,128)(2,1)S(1)}, bf16[1536,1024]{1,0:T(8,128)(2,1)}, u32[]{:S(2)}) copy-start(bf16[1536,1024]{1,0:T(8,128)(2,1)} %get-tuple-element.866) | copy-start | bytes 9437188 | tf_op jit(solution)/shard_map/while
  138.1 12.7 %copy-start.14 = (bf16[128,576]{1,0:T(8,128)(2,1)S(1)}, bf16[128,576]{1,0:T(8,128)(2,1)}, u32[]{:S(2)}) copy-start(bf16[128,576]{1,0:T(8,128)(2,1)} %get-tuple-element.668) | copy-start | bytes 442372 | tf_op jit(solution)/shard_map/while
  138.1 12.6 %copy-start.16 = (bf16[128,544]{1,0:T(8,128)(2,1)S(1)}, bf16[128,544]{1,0:T(8,128)(2,1)}, u32[]{:S(2)}) copy-start(bf16[128,544]{1,0:T(8,128)(2,1)} %get-tuple-element.667) | copy-start | bytes 417796 | tf_op jit(solution)/shard_map/while
  156.9 13.0 %copy-start = (bf16[1536,1024]{1,0:T(8,128)(2,1)S(1)}, bf16[1536,1024]{1,0:T(8,128)(2,1)}, u32[]{:S(2)}) copy-start(bf16[1536,1024]{1,0:T(8,128)(2,1)} %get-tuple-element.866) | copy-start | bytes 9437188 | tf_op jit(solution)/shard_map/while
  188.0 12.7 %copy-start.14 = (bf16[128,576]{1,0:T(8,128)(2,1)S(1)}, bf16[128,576]{1,0:T(8,128)(2,1)}, u32[]{:S(2)}) copy-start(bf16[128,576]{1,0:T(8,128)(2,1)} %get-tuple-element.668) | copy-start | bytes 442372 | tf_op jit(solution)/shard_map/while
  188.0 12.6 %copy-start.16 = (bf16[128,544]{1,0:T(8,128)(2,1)S(1)}, bf16[128,544]{1,0:T(8,128)(2,1)}, u32[]{:S(2)}) copy-start(bf16[128,544]{1,0:T(8,128)(2,1)} %get-tuple-element.667) | copy-start | bytes 417796 | tf_op jit(solution)/shard_map/while
  206.8 13.0 %copy-start = (bf16[1536,1024]{1,0:T(8,128)(2,1)S(1)}, bf16[1536,1024]{1,0:T(8,128)(2,1)}, u32[]{:S(2)}) copy-start(bf16[1536,1024]{1,0:T(8,128)(2,1)} %get-tuple-element.866) | copy-start | bytes 9437188 | tf_op jit(solution)/shard_map/while
  237.9 12.7 %copy-start.14 = (bf16[128,576]{1,0:T(8,128)(2,1)S(1)}, bf16[128,576]{1,0:T(8,128)(2,1)}, u32[]{:S(2)}) copy-start(bf16[128,576]{1,0:T(8,128)(2,1)} %get-tuple-element.668) | copy-start | bytes 442372 | tf_op jit(solution)/shard_map/while
  237.9 12.6 %copy-start.16 = (bf16[128,544]{1,0:T(8,128)(2,1)S(1)}, bf16[128,544]{1,0:T(8,128)(2,1)}, u32[]{:S(2)}) copy-start(bf16[128,544]{1,0:T(8,128)(2,1)} %get-tuple-element.667) | copy-start | bytes 417796 | tf_op jit(solution)/shard_map/while
  276.6 48.1 %copy-start.1 = (bf16[1536,1024]{1,0:T(8,128)(2,1)S(1)}, bf16[1536,1024]{1,0:T(8,128)(2,1)}, u32[]{:S(2)}) copy-start(bf16[1536,1024]{1,0:T(8,128)(2,1)} %get-tuple-element.1109) | copy-start | bytes 9437188
  351.7 12.6 %copy-start.15 = (bf16[128,576]{1,0:T(8,128)(2,1)S(1)}, bf16[128,576]{1,0:T(8,128)(2,1)}, u32[]{:S(2)}) copy-start(bf16[128,576]{1,0:T(8,128)(2,1)} %get-tuple-element.737) | copy-start | bytes 442372 | tf_op jit(solution)/shard_map/while
  351.7 12.6 %copy-start.17 = (bf16[128,544]{1,0:T(8,128)(2,1)S(1)}, bf16[128,544]{1,0:T(8,128)(2,1)}, u32[]{:S(2)}) copy-start(bf16[128,544]{1,0:T(8,128)(2,1)} %get-tuple-element.736) | copy-start | bytes 417796 | tf_op jit(solution)/shard_map/while
  397.6 12.6 %copy-start.15 = (bf16[128,576]{1,0:T(8,128)(2,1)S(1)}, bf16[128,576]{1,0:T(8,128)(2,1)}, u32[]{:S(2)}) copy-start(bf16[128,576]{1,0:T(8,128)(2,1)} %get-tuple-element.737) | copy-start | bytes 442372 | tf_op jit(solution)/shard_map/while
  397.6 12.6 %copy-start.17 = (bf16[128,544]{1,0:T(8,128)(2,1)S(1)}, bf16[128,544]{1,0:T(8,128)(2,1)}, u32[]{:S(2)}) copy-start(bf16[128,544]{1,0:T(8,128)(2,1)} %get-tuple-element.736) | copy-start | bytes 417796 | tf_op jit(solution)/shard_map/while
  443.4 12.6 %copy-start.15 = (bf16[128,576]{1,0:T(8,128)(2,1)S(1)}, bf16[128,576]{1,0:T(8,128)(2,1)}, u32[]{:S(2)}) copy-start(bf16[128,576]{1,0:T(8,128)(2,1)} %get-tuple-element.737) | copy-start | bytes 442372 | tf_op jit(solution)/shard_map/while
  489.2 12.6 %copy-start.15 = (bf16[128,576]{1,0:T(8,128)(2,1)S(1)}, bf16[128,576]{1,0:T(8,128)(2,1)}, u32[]{:S(2)}) copy-start(bf16[128,576]{1,0:T(8,128)(2,1)} %get-tuple-element.737) | copy-start | bytes 442372 | tf_op jit(solution)/shard_map/while
  489.2 12.6 %copy-start.17 = (bf16[128,544]{1,0:T(8,128)(2,1)S(1)}, bf16[128,544]{1,0:T(8,128)(2,1)}, u32[]{:S(2)}) copy-start(bf16[128,544]{1,0:T(8,128)(2,1)} %get-tuple-element.736) | copy-start | bytes 417796 | tf_op jit(solution)/shard_map/while
  (67 other events, 619.7 us)
Sparse Core Ops, SparseCore 0:
  39.3 14.3 all-gather.2
  259.4 10.2 all-gather.4
where the time goes:
time: 520 us; the launch traced here: 518 us
  local copies, waits for them, and re-layouts  381 us (73%)
  blocking collectives  34.8 us (7%)
  matrix products  23.9 us (5%)
  waiting for transfers between devices  22.9 us (4%)
  other arithmetic  21.4 us (4%)
  between operations  14.2 us (3%)
  loops' own time  13.2 us (3%)
  starting transfers between devices  6.27 us (1%)
    while x416, local copies, waits for them, and re-layouts  178 us
    slice x120, local copies, waits for them, and re-layouts, shift_slots(): segment[:, :segment.shape[1] - moved * BLK]  98.7 us
    dynamic_slice x136, local copies, waits for them, and re-layouts, one_group(): lax.dynamic_slice_in_dim(segment, first_slot * BLK, column_slots * BLK, 1)  45.4 us
    psum x1, blocking collectives, per_device(): total_squared = lax.psum(trace_squared, ('row', 'col'))  34.8 us
    dot_general x8, matrix products, one_group(): jnp.einsum('gak,gkn->gan', left_rows, gathered, preferred_element_type=jn...  23.9 us
    ppermute x1, waiting for transfers between devices, extended_2(): before = lax.ppermute(last, axis, up)  21.1 us
    another operation x2, loops' own time, band_part(): lax.map(one_group, jnp.arange(block_rows // group_rows, dtype=jnp.int32))  13.2 us
    transpose x2, other arithmetic, diagonal_sum(): jnp.diagonal(values.reshape(block_rows, BLK, slot_total, BLK), axis1=1, a...  11.4 us
  transfers between devices with their start and end apart: 4, of which 2 were waited for; matrix products, arithmetic and copies ran while one was open for 8% of the time, Pallas kernels for 0%

commit v1 on v0

--- a/solution.py
+++ b/solution.py
@@ -140,7 +140,8 @@
         collect_half,
     )
     trace_squared = diagonal_sum(squared, chosen)
-    total_squared = lax.psum(trace_squared, ("row", "col"))
+    one_axis = lax.psum(trace_squared, "col")
+    total_squared = lax.psum(one_axis, "row")
     order_total = block_total * BLK
     traces = jnp.stack([total_kept, total_squared]) / order_total
     return (purified, traces)

time: 520 us -> 546 us (1.050)
  blocking collectives: 34.8 us -> 55.8 us
    psum x1 -> x3, blocking collectives: 34.8 us -> 55.8 us  [the longest x1 30.3 us: per_device(): total_kept = lax.psum(trace_kept, ('row', 'col'))]
where the time goes in v1:
time: 546 us; the launch traced here: 544 us
  local copies, waits for them, and re-layouts  386 us (71%)
  blocking collectives  55.8 us (10%)
  matrix products  23.9 us (4%)
  waiting for transfers between devices  22.9 us (4%)
  other arithmetic  21.3 us (4%)
  between operations  14.2 us (3%)
  loops' own time  13.2 us (2%)
  starting transfers between devices  6.27 us (1%)
    while x416, local copies, waits for them, and re-layouts  182 us
    slice x120, local copies, waits for them, and re-layouts, shift_slots(): segment[:, :segment.shape[1] - moved * BLK]  99.2 us
    dynamic_slice x136, local copies, waits for them, and re-layouts, one_group(): lax.dynamic_slice_in_dim(segment, first_slot * BLK, column_slots * BLK, 1)  45.5 us
    psum x1, blocking collectives, per_device(): total_kept = lax.psum(trace_kept, ('row', 'col'))  30.3 us
    dot_general x8, matrix products, one_group(): jnp.einsum('gak,gkn->gan', left_rows, gathered, preferred_element_type=jn...  23.9 us
    psum x1, blocking collectives, per_device(): total_squared = lax.psum(one_axis, 'row')  22.3 us
    ppermute x1, waiting for transfers between devices, extended_2(): before = lax.ppermute(last, axis, up)  21.1 us
    another operation x2, loops' own time, band_part(): lax.map(one_group, jnp.arange(block_rows // group_rows, dtype=jnp.int32))  13.2 us
  transfers between devices with their start and end apart: 4, of which 2 were waited for; matrix products, arithmetic and copies ran while one was open for 8% of the time, Pallas kernels for 0%

profile of v1, /device:TPU:0, one launch (start us, length us, event | category | flops | bytes accessed | tf_op | source)
XLA Modules:
  0.0 543.8 jit_solution(13312325032449988135)
XLA Ops:
  10.6 4.9 collective-permute-start
  16.8 21.1 %collective-permute-done = bf16[512,512]{1,0:T(8,128)(2,1)S(1)} collective-permute-done((bf16[512,512]{1,0:T(8,128)(2,1)S(1)}, bf16[512,512]{1,0:T(8,128)(2,1)S(1)}, u32[]{:S(2)}, u32[]{:S(2)}) %collective-permute-start) | collective-permute-done | bytes 524320 | tf_op jit(solution)/shard_map/ppermute | solution.py:16
  40.5 4.3 copy.7
  47.1 4.7 mul.809
  57.1 203.0 %while.26 = (s32[]{:T(128)}, f32[4,128,512]{2,1,0:T(8,128)}, s32[4]{0:T(128)S(1)}, bf16[512,1024]{1,0:T(8,128)(2,1)}, bf16[1536,1024]{1,0:T(8,128)(2,1)}, /*inde...) while((s32[]{:T(128)}, f32[4,128,512]{2,1,0:T(8,128)}, ...), condition=%wide.region_1.2_spmd, body=%wide.region_0.1_spmd.sunk | while | flops 134217904 | bytes 56200764 | solution.py:83
  104.1 3.0 fusion.27
  154.8 3.0 fusion.27
  205.6 3.0 fusion.27
  256.3 3.0 fusion.27
  262.6 4.6 multiply_bitcast_fusion
  267.2 2.8 gather_fusion
  270.0 2.7 reshape_reshape.10
  272.7 7.3 %copy.8 = f32[16,32,16,32]{2,0,3,1:T(8,128)} copy(f32[16,32,16,32]{3,2,1,0:T(8,128)} %reshape_reshape.10) | data formatting | bytes 2097152 | tf_op jit(solution)/shard_map/reshape;reshape | solution.py:32
  280.0 6.8 %fusion = bf16[16,16,32,32]{1,0,3,2:T(8,128)(2,1)} fusion(f32[16,32,16,32]{2,0,3,1:T(8,128)} %copy.8, f32[16,16]{1,0:T(8,128)S(1)} %get-tuple-element.401), kind=kLoop, calls=%fused_computation.163 | loop fusion | flops 524288 | bytes 1573888 | tf_op jit(solution)/shard_map/jit(diagonal)/transpose | solution.py:90
  286.8 2.8 gather_fusion.1
  290.3 3.2 psum.22
  293.5 22.3 %psum.23 = f32[1]{0:T(128)} all-reduce(f32[1]{0:T(128)} %bitcast.140), channel_id=1, replica_groups=mesh['snap'=2,'row'=8,'col'=2] {'row'}, use_global_device_ids=true, to_apply=%region_8.9 | all-reduce | flops 1 | bytes 8 | tf_op jit(solution)/shard_map/psum | solution.py:144
  315.7 30.3 %psum.21 = f32[1]{0:T(128)} all-reduce(f32[1]{0:T(128)} %bitcast.138), channel_id=1, replica_groups=mesh['snap'=2,'row'=8,'col'=2] {'row','col'}, use_global_device_ids=true, to_apply=%region_5.6 | all-reduce | flops 1 | bytes 8 | tf_op jit(solution)/shard_map/psum | solution.py:123
  349.0 185.2 %while.27 = (s32[]{:T(128)}, f32[4,128,512]{2,1,0:T(8,128)}, s32[4]{0:T(128)S(1)}, bf16[512,1024]{1,0:T(8,128)(2,1)}, bf16[1536,1024]{1,0:T(8,128)(2,1)S(1)}, /*...) while((s32[]{:T(128)}, f32[4,128,512]{2,1,0:T(8,128)}, ...), condition=%wide.region_3.4_spmd, body=%wide.region_2.3_spmd.sunk | while | flops 134217904 | bytes 43617860 | solution.py:83
  391.6 3.0 fusion.31
  437.9 3.0 fusion.31
  484.2 3.0 fusion.31
  530.5 3.0 fusion.31
  534.2 2.8 fusion.3
  (736 shorter events, 372.0 us)
Async XLA Ops:
  7.2 46.5 %all-gather.3.cloned.1.call-start = ((), (), s32[]{:S(2)}) async-start(), calls=%async_computation | async-start | bytes 4718592 | tf_op jit(solution)/shard_map/all_gather | solution.py:126
  10.6 27.3 %collective-permute-start = (bf16[512,512]{1,0:T(8,128)(2,1)S(1)}, bf16[512,512]{1,0:T(8,128)(2,1)S(1)}, u32[]{:S(2)}, u32[]{:S(2)}) collective-permute-start(bf16[512,512]{1,0:T(8,128)(2,1)S(1)} %mul.805), channel_id=1, source_target_pairs={{0,2},{2,4},{4,6},{6,8},{8,10},{10,12},{12,14},{1,3},{3,5},{5,7},{... | collective-permute-start | bytes 1572872 | tf_op jit(solution)/shard_map/ppermute | solution.py:16
  15.5 22.4 %collective-permute-start.1 = (bf16[512,512]{1,0:T(8,128)(2,1)S(1)}, bf16[512,512]{1,0:T(8,128)(2,1)S(1)}, u32[]{:S(2)}, u32[]{:S(2)}) collective-permute-start(bf16[512,512]{1,0:T(8,128)(2,1)S(1)} %mul.805), channel_id=1, source_target_pairs={{2,0},{4,2},{6,4},{8,6},{10,8},{12,10},{14,12},{3,1},{5,3},{7,5},{... | collective-permute-start | bytes 1572872 | tf_op jit(solution)/shard_map/ppermute | solution.py:17
  39.2 308.7 %all-gather.5.cloned.1.call-start = ((), (), s32[]{:S(2)}) async-start(), calls=%async_computation.1 | async-start | bytes 1572864 | tf_op jit(solution)/shard_map/all_gather | solution.py:130
  57.1 13.3 %copy-start = (bf16[1536,1024]{1,0:T(8,128)(2,1)S(1)}, bf16[1536,1024]{1,0:T(8,128)(2,1)}, u32[]{:S(2)}) copy-start(bf16[1536,1024]{1,0:T(8,128)(2,1)} %get-tuple-element.864) | copy-start | bytes 9437188 | tf_op jit(solution)/shard_map/while
  88.6 12.9 %copy-start.14 = (bf16[128,576]{1,0:T(8,128)(2,1)S(1)}, bf16[128,576]{1,0:T(8,128)(2,1)}, u32[]{:S(2)}) copy-start(bf16[128,576]{1,0:T(8,128)(2,1)} %get-tuple-element.666) | copy-start | bytes 442372 | tf_op jit(solution)/shard_map/while
  88.7 12.9 %copy-start.16 = (bf16[128,544]{1,0:T(8,128)(2,1)S(1)}, bf16[128,544]{1,0:T(8,128)(2,1)}, u32[]{:S(2)}) copy-start(bf16[128,544]{1,0:T(8,128)(2,1)} %get-tuple-element.665) | copy-start | bytes 417796 | tf_op jit(solution)/shard_map/while
  107.8 13.3 %copy-start = (bf16[1536,1024]{1,0:T(8,128)(2,1)S(1)}, bf16[1536,1024]{1,0:T(8,128)(2,1)}, u32[]{:S(2)}) copy-start(bf16[1536,1024]{1,0:T(8,128)(2,1)} %get-tuple-element.864) | copy-start | bytes 9437188 | tf_op jit(solution)/shard_map/while
  139.4 12.9 %copy-start.14 = (bf16[128,576]{1,0:T(8,128)(2,1)S(1)}, bf16[128,576]{1,0:T(8,128)(2,1)}, u32[]{:S(2)}) copy-start(bf16[128,576]{1,0:T(8,128)(2,1)} %get-tuple-element.666) | copy-start | bytes 442372 | tf_op jit(solution)/shard_map/while
  139.4 12.9 %copy-start.16 = (bf16[128,544]{1,0:T(8,128)(2,1)S(1)}, bf16[128,544]{1,0:T(8,128)(2,1)}, u32[]{:S(2)}) copy-start(bf16[128,544]{1,0:T(8,128)(2,1)} %get-tuple-element.665) | copy-start | bytes 417796 | tf_op jit(solution)/shard_map/while
  158.6 13.3 %copy-start = (bf16[1536,1024]{1,0:T(8,128)(2,1)S(1)}, bf16[1536,1024]{1,0:T(8,128)(2,1)}, u32[]{:S(2)}) copy-start(bf16[1536,1024]{1,0:T(8,128)(2,1)} %get-tuple-element.864) | copy-start | bytes 9437188 | tf_op jit(solution)/shard_map/while
  190.1 12.9 %copy-start.14 = (bf16[128,576]{1,0:T(8,128)(2,1)S(1)}, bf16[128,576]{1,0:T(8,128)(2,1)}, u32[]{:S(2)}) copy-start(bf16[128,576]{1,0:T(8,128)(2,1)} %get-tuple-element.666) | copy-start | bytes 442372 | tf_op jit(solution)/shard_map/while
  190.2 12.9 %copy-start.16 = (bf16[128,544]{1,0:T(8,128)(2,1)S(1)}, bf16[128,544]{1,0:T(8,128)(2,1)}, u32[]{:S(2)}) copy-start(bf16[128,544]{1,0:T(8,128)(2,1)} %get-tuple-element.665) | copy-start | bytes 417796 | tf_op jit(solution)/shard_map/while
  209.3 13.3 %copy-start = (bf16[1536,1024]{1,0:T(8,128)(2,1)S(1)}, bf16[1536,1024]{1,0:T(8,128)(2,1)}, u32[]{:S(2)}) copy-start(bf16[1536,1024]{1,0:T(8,128)(2,1)} %get-tuple-element.864) | copy-start | bytes 9437188 | tf_op jit(solution)/shard_map/while
  240.9 12.9 %copy-start.14 = (bf16[128,576]{1,0:T(8,128)(2,1)S(1)}, bf16[128,576]{1,0:T(8,128)(2,1)}, u32[]{:S(2)}) copy-start(bf16[128,576]{1,0:T(8,128)(2,1)} %get-tuple-element.666) | copy-start | bytes 442372 | tf_op jit(solution)/shard_map/while
  240.9 12.9 %copy-start.16 = (bf16[128,544]{1,0:T(8,128)(2,1)S(1)}, bf16[128,544]{1,0:T(8,128)(2,1)}, u32[]{:S(2)}) copy-start(bf16[128,544]{1,0:T(8,128)(2,1)} %get-tuple-element.665) | copy-start | bytes 417796 | tf_op jit(solution)/shard_map/while
  280.0 69.0 %copy-start.1 = (bf16[1536,1024]{1,0:T(8,128)(2,1)S(1)}, bf16[1536,1024]{1,0:T(8,128)(2,1)}, u32[]{:S(2)}) copy-start(bf16[1536,1024]{1,0:T(8,128)(2,1)} %get-tuple-element.1107) | copy-start | bytes 9437188
  376.2 12.9 %copy-start.15 = (bf16[128,576]{1,0:T(8,128)(2,1)S(1)}, bf16[128,576]{1,0:T(8,128)(2,1)}, u32[]{:S(2)}) copy-start(bf16[128,576]{1,0:T(8,128)(2,1)} %get-tuple-element.735) | copy-start | bytes 442372 | tf_op jit(solution)/shard_map/while
  376.2 12.9 %copy-start.17 = (bf16[128,544]{1,0:T(8,128)(2,1)S(1)}, bf16[128,544]{1,0:T(8,128)(2,1)}, u32[]{:S(2)}) copy-start(bf16[128,544]{1,0:T(8,128)(2,1)} %get-tuple-element.734) | copy-start | bytes 417796 | tf_op jit(solution)/shard_map/while
  422.5 12.9 %copy-start.15 = (bf16[128,576]{1,0:T(8,128)(2,1)S(1)}, bf16[128,576]{1,0:T(8,128)(2,1)}, u32[]{:S(2)}) copy-start(bf16[128,576]{1,0:T(8,128)(2,1)} %get-tuple-element.735) | copy-start | bytes 442372 | tf_op jit(solution)/shard_map/while
  422.5 12.9 %copy-start.17 = (bf16[128,544]{1,0:T(8,128)(2,1)S(1)}, bf16[128,544]{1,0:T(8,128)(2,1)}, u32[]{:S(2)}) copy-start(bf16[128,544]{1,0:T(8,128)(2,1)} %get-tuple-element.734) | copy-start | bytes 417796 | tf_op jit(solution)/shard_map/while
  468.8 12.9 %copy-start.15 = (bf16[128,576]{1,0:T(8,128)(2,1)S(1)}, bf16[128,576]{1,0:T(8,128)(2,1)}, u32[]{:S(2)}) copy-start(bf16[128,576]{1,0:T(8,128)(2,1)} %get-tuple-element.735) | copy-start | bytes 442372 | tf_op jit(solution)/shard_map/while
  468.8 12.9 %copy-start.17 = (bf16[128,544]{1,0:T(8,128)(2,1)S(1)}, bf16[128,544]{1,0:T(8,128)(2,1)}, u32[]{:S(2)}) copy-start(bf16[128,544]{1,0:T(8,128)(2,1)} %get-tuple-element.734) | copy-start | bytes 417796 | tf_op jit(solution)/shard_map/while
  515.1 12.9 %copy-start.15 = (bf16[128,576]{1,0:T(8,128)(2,1)S(1)}, bf16[128,576]{1,0:T(8,128)(2,1)}, u32[]{:S(2)}) copy-start(bf16[128,576]{1,0:T(8,128)(2,1)} %get-tuple-element.735) | copy-start | bytes 442372 | tf_op jit(solution)/shard_map/while
  (67 other events, 630.1 us)
Sparse Core Ops, SparseCore 0:
  39.3 14.3 all-gather.2
  262.7 10.2 all-gather.4
